TPU v7x, 32 devices: a whole 2x2x4 slice. The times are simulated.
32 devices in a mesh: grp: 16 (over z, y, core), col: 2 (over x).
Axes of the slice: x: 2, y: 2, z: 4, core: 2. Of those that a mesh axis runs over, the one named last changes fastest.
Arguments:
- grad: float32 [4096, 16384], P('col', 'grp'), may hold values from -1.8 to 1.8
- exp_avg: float32 [4096, 16384], P('col', 'grp'), may hold values from -1.8 to 1.8
- exp_avg_sq: float32 [4096, 16384], P('col', 'grp'), may hold values from 0.01 to 0.36
- left_basis: bfloat16 [4096, 4096], P('grp', 'col'), may hold values from -1 to 1
- right_basis: bfloat16 [16384, 512], P('grp', 'col'), may hold values from -1 to 1
- gram_left: float32 [4096, 4096], P('grp', 'col'), may hold values from -6 to 6
- gram_right: float32 [16384, 512], P('grp', 'col'), may hold values from -6 to 6
Outputs:
- update: float32 [4096, 16384], P('col', 'grp')
- first_moment: float32 [4096, 16384], P('col', 'grp')
- second_moment: float32 [4096, 16384], P('col', 'grp')
- left_stat: float32 [4096, 4096], P('grp', 'col')
- right_stat: float32 [16384, 512], P('grp', 'col')
All inputs are finite; a program needn't handle non-finite values.
Results may differ from a plain program's by a relative error of at most 0.0041.
Values may be sent and summed in bfloat16 or wider, within the bound.
No kernel may reach another device: no remote copies, remote signals or barrier semaphores. Data moves between devices by JAX's collectives and lax.ppermute only.
A program may use at most 256 MiB of HBM per device.

v0:
```python
import jax
import jax.numpy as jnp
from jax import lax
from jax.sharding import PartitionSpec as P

RB = 512
decay = 0.95
bias_fix = 1.0 - decay**10


def local(grad, exp_avg, exp_avg_sq, left_basis, right_basis, gram_left, gram_right):
    col_count = lax.axis_size("col")
    rows_here, cols_here = grad.shape
    block_count = cols_here // RB
    rounded = grad.astype(jnp.bfloat16)
    panels = lax.all_gather(right_basis, "col", axis=1, tiled=True)
    blocks = panels.reshape(block_count, RB, RB)
    gathered = lax.all_gather(rounded, "col", axis=0, tiled=True)
    height = gathered.shape[0]
    product = jnp.einsum(
        "mbj,bjr->mbr",
        gathered.reshape(height, block_count, RB),
        blocks,
        preferred_element_type=jnp.float32,
    )
    turned = product.reshape(height, cols_here).astype(jnp.bfloat16)
    left_cols = lax.all_gather(left_basis, "grp", axis=0, tiled=True)
    rotated = lax.dot_general(
        left_cols, turned, (((0,), (0,)), ((), ())), preferred_element_type=jnp.float32
    )
    first_moment = decay * exp_avg + (1.0 - decay) * rotated
    second_moment = decay * exp_avg_sq + (1.0 - decay) * rotated * rotated
    direction = (first_moment / bias_fix / (jnp.sqrt(second_moment / bias_fix) + 1e-08)).astype(
        jnp.bfloat16
    )
    left_rows = lax.all_to_all(left_cols, "col", split_axis=0, concat_axis=1, tiled=True)
    back = jnp.dot(
        left_rows,
        lax.all_gather(direction, "col", axis=0, tiled=True),
        preferred_element_type=jnp.float32,
    )
    back = back.astype(jnp.bfloat16)
    update = jnp.einsum(
        "mbr,bjr->mbj",
        back.reshape(rows_here, block_count, RB),
        blocks,
        preferred_element_type=jnp.float32,
    )
    update = update.reshape(rows_here, cols_here)
    left_term = lax.psum_scatter(
        lax.dot_general(
            gathered, rounded, (((1,), (1,)), ((), ())), preferred_element_type=jnp.float32
        ),
        "grp",
        scatter_dimension=0,
        tiled=True,
    )
    left_stat = decay * gram_left + (1.0 - decay) * left_term
    share = RB // col_count
    offset = lax.axis_index("col") * share
    whole_blocks = gathered.reshape(gathered.shape[0], block_count, RB)
    narrow = lax.dynamic_slice_in_dim(whole_blocks, offset, share, 2)
    right_term = jnp.einsum(
        "mbj,mbr->bjr", whole_blocks, narrow, preferred_element_type=jnp.float32
    )
    right_stat = decay * gram_right + (1.0 - decay) * right_term.reshape(cols_here, share)
    return (update, first_moment, second_moment, left_stat, right_stat)


def solution(mesh):
    return jax.shard_map(
        local,
        mesh=mesh,
        in_specs=(
            P("col", "grp"),
            P("col", "grp"),
            P("col", "grp"),
            P("grp", "col"),
            P("grp", "col"),
            P("grp", "col"),
            P("grp", "col"),
        ),
        out_specs=(
            P("col", "grp"),
            P("col", "grp"),
            P("col", "grp"),
            P("grp", "col"),
            P("grp", "col"),
        ),
        check_vma=False,
    )
```

profile of v0, /device:TPU:0, one launch (start us, length us, event | category | flops | bytes accessed | tf_op | source)
XLA Modules:
  0.0 815.0 jit_solution(15229390837524339780)
XLA Ops:
  7.2 0.0 all-gather.5.cloned.1.call-start
  7.2 0.7 all-gather.5.cloned.1.call-update
  7.9 0.0 all-gather.7.cloned.1.call-start
  7.9 7.3 copy.32
  15.3 0.0 all-gather.7.cloned.1.call-update
  15.3 0.0 all-gather.9.cloned.1.call-start
  15.4 0.7 all-gather.9.cloned.1.call-update
  16.0 0.0 all-gather.11.cloned.1.call-start
  16.1 9.2 %copy.31 = f32[2048,1024]{0,1:T(8,128)} copy(f32[2048,1024]{1,0:T(8,128)} %param.8) | data formatting | bytes 16777216 | tf_op args[1]
  25.3 9.1 %copy.35 = f32[2048,1024]{0,1:T(8,128)} copy(f32[2048,1024]{1,0:T(8,128)} %param.9) | data formatting | bytes 16777216 | tf_op args[2]
  34.4 0.0 all-gather.5.cloned.1.call-done
  34.4 104.7 %all-gather.7.cloned.1.call-done = bf16[4096,1024]{0,1:T(8,128)(2,1)} async-done(((bf16[2048,1024]{0,1:T(8,128)(2,1)}), bf16[4096,1024]{0,1:T(8,128)(2,1)}) %all-gather.7.cloned.1.call-update) | async-done | bytes 8388624 | tf_op jit(solution)/shard_map/all_gather | solution.py:18
  139.1 12.1 %convolution_convert_fusion = bf16[2,512,4096]{2,1,0:T(8,128)(2,1)} fusion(bf16[2,512,512]{2,1,0:T(8,128)(2,1)} %bitcast.38, bf16[4096,2,512]{0,2,1:T(8,128)(2,1)} %bitcast.40), kind=kOutput, calls=%fused_computation.4 | convolution fusion | flops 4299161600 | bytes 17825792 | tf_op jit(solution)/shard_map/mbj,bjr->mbr/dot_general | solution.py:20
  151.2 116.5 %all-gather.9.cloned.1.call-done = bf16[4096,2048]{1,0:T(8,128)(2,1)} async-done(((bf16[256,2048]{1,0:T(8,128)(2,1)}), bf16[4096,2048]{1,0:T(8,128)(2,1)}) %all-gather.9.cloned.1.call-update) | async-done | bytes 16777232 | tf_op jit(solution)/shard_map/all_gather | solution.py:27
  267.7 33.8 %divide_convert_fusion = (bf16[2048,1024]{0,1:T(8,128)(2,1)}, f32[2048,1024]{0,1:T(8,128)}, f32[2048,1024]{0,1:T(8,128)}) fusion(f32[2048,1024]{0,1:T(8,128)} %copy.31, f32[2048,1024]{0,1:T(8,128)} %copy.35, bf16[4096,1024]{0,1:T(8,128)(2,1)} %bitcast.42, bf16[4096,2048]{1,0:T(8,128)(2,1)} %all-gather.9.cloned.1.call-done), kind=kOutput, calls=%fused_computation.3 | convolution fusion | flops 17202937856 | bytes 62914560 | tf_op jit(solution)/shard_map/dot_general | solution.py:28
  301.5 0.0 all-gather.11.cloned.1.call-update
  301.5 0.2 reduce-scatter.2.cloned.1.call-start
  301.7 25.6 %fusion.11 = f32[4096,2048]{1,0:T(8,128)} fusion(bf16[4096,1024]{0,1:T(8,128)(2,1)} %all-gather.7.cloned.1.call-done, bf16[2048,1024]{0,1:T(8,128)(2,1)} %copy.32), kind=kOutput, calls=%fused_computation.13 | convolution fusion | flops 17179869184 | bytes 46137344 | tf_op jit(solution)/shard_map/dot_general | solution.py:51
  327.3 0.0 reduce-scatter.2.cloned.1.call-update
  327.3 9.7 %all-to-all-start = ((bf16[2,2048,2048]{2,1,0:T(8,128)(2,1)}), bf16[2,2048,2048]{2,1,0:T(8,128)(2,1)}, u32[]{:S(2)}, u32[]{:S(2)}) async-start(bf16[2,2048,2048]{2,1,0:T(8,128)(2,1)} %bitcast.35), calls=%async_computation | async-start | bytes 33554432 | tf_op jit(solution)/shard_map/all_to_all | solution.py:36
  337.0 0.0 copy-start.2
  337.1 7.1 fusion.6
  344.2 0.3 copy.39
  344.5 0.0 copy-done.2
  344.5 1.1 bitcast_add_fusion
  345.6 9.2 %copy.41 = f32[2048,1024]{1,0:T(8,128)} copy(f32[2048,1024]{0,1:T(8,128)} %get-tuple-element.21) | data formatting | bytes 16777216
  354.9 9.2 %copy.42 = f32[2048,1024]{1,0:T(8,128)} copy(f32[2048,1024]{0,1:T(8,128)} %get-tuple-element.22) | data formatting | bytes 16777216
  364.1 219.3 %all-to-all-done = bf16[2,2048,2048]{2,1,0:T(8,128)(2,1)} async-done(((bf16[2,2048,2048]{2,1,0:T(8,128)(2,1)}), bf16[2,2048,2048]{2,1,0:T(8,128)(2,1)}, u32[]{:S(2)}, u32[]{:S(2)}) %all-to-all-start) | async-done | bytes 16777248 | tf_op jit(solution)/shard_map/all_to_all | solution.py:36
  583.4 22.8 %copy.36 = bf16[2048,2,2048]{0,2,1:T(8,128)(2,1)} copy(bf16[2048,2,2048]{2,0,1:T(8,128)(2,1)} %bitcast.6) | data formatting | bytes 33554432 | tf_op jit(solution)/shard_map/all_to_all | solution.py:36
  606.2 0.0 all-gather.11.cloned.1.call-done
  606.2 0.0 copy-start
  606.2 22.8 %convolution_convert_fusion.1 = bf16[1024,2048]{1,0:T(8,128)(2,1)S(1)} fusion(bf16[4096,1024]{0,1:T(8,128)(2,1)} %all-gather.11.cloned.1.call-done, bf16[2048,4096]{0,1:T(8,128)(2,1)} %bitcast.36), kind=kOutput, calls=%fused_computation.7 | convolution fusion | flops 17181966336 | bytes 29360128 | tf_op jit(solution)/shard_map/dot_general | solution.py:37
  629.0 0.0 copy-done
  629.0 5.6 fusion.12
  634.6 0.0 copy-start.1
  634.6 9.4 %copy.40 = f32[2048,1024]{1,0:T(8,128)} copy(f32[2048,1024]{0,1:T(8,128)} %bitcast.34) | data formatting | bytes 16777216
  644.0 161.2 %reduce-scatter.2.cloned.1.call-done = f32[256,2048]{1,0:T(8,128)} async-done(((f32[4096,2048]{1,0:T(8,128)}), f32[256,2048]{1,0:T(8,128)}) %reduce-scatter.2.cloned.1.call-update) | async-done | bytes 2097168 | tf_op jit(solution)/shard_map/reduce_scatter | solution.py:50
  805.2 0.0 copy-done.1
  805.2 3.3 multiply_add_fusion.1
Async XLA Ops:
  7.2 27.2 %all-gather.5.cloned.1.call-start = ((), (), s32[]{:S(2)}) async-start(), calls=%async_computation.2 | async-start | bytes 1572864 | tf_op jit(solution)/shard_map/all_gather | solution.py:16
  7.9 131.2 %all-gather.7.cloned.1.call-start = ((), (), s32[]{:S(2)}) async-start(), calls=%async_computation.3 | async-start | bytes 12582912 | tf_op jit(solution)/shard_map/all_gather | solution.py:18
  15.3 252.4 %all-gather.9.cloned.1.call-start = ((), (), s32[]{:S(2)}) async-start(), calls=%async_computation.4 | async-start | bytes 17825792 | tf_op jit(solution)/shard_map/all_gather | solution.py:27
  16.0 590.2 %all-gather.11.cloned.1.call-start = ((), (), s32[]{:S(2)}) async-start(), calls=%async_computation.5 | async-start | bytes 12582912 | tf_op jit(solution)/shard_map/all_gather | solution.py:39
  301.5 503.7 %reduce-scatter.2.cloned.1.call-start = ((), (), s32[]{:S(2)}) async-start(), calls=%async_computation.6 | async-start | bytes 35651584 | tf_op jit(solution)/shard_map/reduce_scatter | solution.py:50
  327.3 256.1 %all-to-all-start = ((bf16[2,2048,2048]{2,1,0:T(8,128)(2,1)}), bf16[2,2048,2048]{2,1,0:T(8,128)(2,1)}, u32[]{:S(2)}, u32[]{:S(2)}) async-start(bf16[2,2048,2048]{2,1,0:T(8,128)(2,1)} %bitcast.35), calls=%async_computation | async-start | bytes 33554432 | tf_op jit(solution)/shard_map/all_to_all | solution.py:36
  337.0 7.5 copy-start.2
  606.2 22.8 %copy-start = (bf16[1024,512]{1,0:T(8,128)(2,1)S(1)}, bf16[1024,512]{1,0:T(8,128)(2,1)}, u32[]{:S(2)}) copy-start(bf16[1024,512]{1,0:T(8,128)(2,1)} %all-gather.5.cloned.1.call-done) | copy-start | bytes 3145732
  634.6 170.6 %copy-start.1 = (f32[256,2048]{1,0:T(8,128)S(1)}, f32[256,2048]{1,0:T(8,128)}, u32[]{:S(2)}) copy-start(f32[256,2048]{1,0:T(8,128)} %param.12) | copy-start | bytes 6291460
Sparse Core Ops, SparseCore 0:
  9.5 23.9 all-gather.4
  35.0 103.9 all-gather.6
  141.2 126.4 all-gather.8
  301.6 165.6 all-gather.10
  471.4 333.7 reduce-scatter.1
where the time goes:
time: 816 us; the launch traced here: 815 us
  waiting for transfers between devices  603 us (74%)
  matrix products  107 us (13%)
  local copies, waits for them, and re-layouts  76.7 us (9%)
  between operations  13.8 us (2%)
  starting transfers between devices  10.1 us (1%)
    all_to_all x1, waiting for transfers between devices, local(): lax.all_to_all(left_cols, 'col', split_axis=0, concat_axis=1, tiled=True)  219 us
    reduce_scatter x1, waiting for transfers between devices, local(): lax.psum_scatter(lax.dot_general(gathered, rounded, (((1,), (1,)), ((), (...  161 us
    all_gather x1, waiting for transfers between devices, local(): left_cols = lax.all_gather(left_basis, 'grp', axis=0, tiled=True)  117 us
    all_gather x1, waiting for transfers between devices, local(): gathered = lax.all_gather(rounded, 'col', axis=0, tiled=True)  105 us
    unnamed x12, local copies, waits for them, and re-layouts  53.5 us
    dot_general x1, matrix products, local(): lax.dot_general(left_cols, turned, (((0,), (0,)), ((), ())), preferred_el...  33.8 us
    dot_general x1, matrix products, local(): lax.dot_general(gathered, rounded, (((1,), (1,)), ((), ())), preferred_el...  25.6 us
    all_to_all x1, local copies, waits for them, and re-layouts, local(): lax.all_to_all(left_cols, 'col', split_axis=0, concat_axis=1, tiled=True)  22.8 us
  transfers between devices with their start and end apart: 6, of which 4 were waited for; matrix products, arithmetic and copies ran while one was open for 19% of the time, Pallas kernels for 0%

commit v1 on v0

--- a/solution.py
+++ b/solution.py
@@ -24,7 +24,12 @@
         preferred_element_type=jnp.float32,
     )
     turned = product.reshape(height, cols_here).astype(jnp.bfloat16)
-    left_cols = lax.all_gather(left_basis, "grp", axis=0, tiled=True)
+    ring = [left_basis]
+    for hop in range(15):
+        ring.append(lax.ppermute(ring[-1], "grp", [(dev, (dev + 1) % 16) for dev in range(16)]))
+    left_cols = jnp.roll(
+        jnp.concatenate(ring[::-1], axis=0), (lax.axis_index("grp") + 1) * ring[0].shape[0], axis=0
+    )
     rotated = lax.dot_general(
         left_cols, turned, (((0,), (0,)), ((), ())), preferred_element_type=jnp.float32
     )

time: 816 us -> 866 us (1.061)
  waiting for transfers between devices: 603 us -> 657 us
    ppermute x0 -> x15, waiting for transfers between devices: none -> 237 us  [local(): lax.ppermute(ring[-1], 'grp', [(dev, (dev + 1) % 16) for dev in range(16)])]
    all_gather x1 -> x0, waiting for transfers between devices: 117 us -> none  [local(): left_cols = lax.all_gather(left_basis, 'grp', axis=0, tiled=True)]
    all_gather x1, waiting for transfers between devices: 105 us -> 0.01 us  [local(): gathered = lax.all_gather(rounded, 'col', axis=0, tiled=True)]
    reduce_scatter x1, waiting for transfers between devices: 161 us -> 184 us  [local(): lax.psum_scatter(lax.dot_general(gathered, rounded, (((1,), (1,)), ((), (...]
    all_to_all x1, waiting for transfers between devices: 219 us -> 237 us  [local(): lax.all_to_all(left_cols, 'col', split_axis=0, concat_axis=1, tiled=True)]
    unnamed x12 -> x69, local copies, waits for them, and re-layouts: 53.5 us -> 39.5 us
  transfers between devices with their start and end apart: 6 -> 20, of which waited for: 4 -> 17; matrix products, arithmetic and copies ran while one was open for 19% -> 13% of each run, Pallas kernels for 0% -> 0%
where the time goes in v1:
time: 866 us; the launch traced here: 865 us
  waiting for transfers between devices  657 us (76%)
  matrix products  109 us (13%)
  local copies, waits for them, and re-layouts  69.5 us (8%)
  between operations  14.2 us (2%)
  starting transfers between devices  10.6 us (1%)
    all_to_all x1, waiting for transfers between devices, local(): lax.all_to_all(left_cols, 'col', split_axis=0, concat_axis=1, tiled=True)  237 us
    ppermute x15, waiting for transfers between devices, local(): lax.ppermute(ring[-1], 'grp', [(dev, (dev + 1) % 16) for dev in range(16)])  237 us
    reduce_scatter x1, waiting for transfers between devices, local(): lax.psum_scatter(lax.dot_general(gathered, rounded, (((1,), (1,)), ((), (...  184 us
    unnamed x69, local copies, waits for them, and re-layouts  39.5 us
    dot_general x1, matrix products, local(): lax.dot_general(left_cols, turned, (((0,), (0,)), ((), ())), preferred_el...  35.4 us
    dot_general x1, matrix products, local(): lax.dot_general(gathered, rounded, (((1,), (1,)), ((), ())), preferred_el...  25.8 us
    dot_general x1, matrix products, local(): jnp.dot(left_rows, lax.all_gather(direction, 'col', axis=0, tiled=True),...  23 us
    all_to_all x1, local copies, waits for them, and re-layouts, local(): lax.all_to_all(left_cols, 'col', split_axis=0, concat_axis=1, tiled=True)  22.6 us
  transfers between devices with their start and end apart: 20, of which 17 were waited for; matrix products, arithmetic and copies ran while one was open for 13% of the time, Pallas kernels for 0%

profile of v1, /device:TPU:0, one launch (start us, length us, event | category | flops | bytes accessed | tf_op | source)
XLA Modules:
  0.0 864.6 jit_solution(6327275457030166406)
XLA Ops:
  7.8 17.7 %collective-permute-done = bf16[256,2048]{1,0:T(8,128)(2,1)S(1)} collective-permute-done((bf16[256,2048]{1,0:T(8,128)(2,1)}, bf16[256,2048]{1,0:T(8,128)(2,1)S(1)}, u32[]{:S(2)}, u32[]{:S(2)}) %collective-permute-start) | collective-permute-done | bytes 1048608 | tf_op jit(solution)/shard_map/ppermute | solution.py:29
  25.4 16.9 %collective-permute-done.1 = bf16[256,2048]{1,0:T(8,128)(2,1)S(1)} collective-permute-done((bf16[256,2048]{1,0:T(8,128)(2,1)S(1)}, bf16[256,2048]{1,0:T(8,128)(2,1)S(1)}, u32[]{:S(2)}, u32[]{:S(2)}) %collective-permute-start.1) | collective-permute-done | bytes 1048608 | tf_op jit(solution)/shard_map/ppermute | solution.py:29
  42.4 16.9 %collective-permute-done.2 = bf16[256,2048]{1,0:T(8,128)(2,1)S(1)} collective-permute-done((bf16[256,2048]{1,0:T(8,128)(2,1)S(1)}, bf16[256,2048]{1,0:T(8,128)(2,1)S(1)}, u32[]{:S(2)}, u32[]{:S(2)}) %collective-permute-start.2) | collective-permute-done | bytes 1048608 | tf_op jit(solution)/shard_map/ppermute | solution.py:29
  59.3 16.9 %collective-permute-done.3 = bf16[256,2048]{1,0:T(8,128)(2,1)S(1)} collective-permute-done((bf16[256,2048]{1,0:T(8,128)(2,1)S(1)}, bf16[256,2048]{1,0:T(8,128)(2,1)S(1)}, u32[]{:S(2)}, u32[]{:S(2)}) %collective-permute-start.3) | collective-permute-done | bytes 1048608 | tf_op jit(solution)/shard_map/ppermute | solution.py:29
  76.2 1.0 copy-done.1
  77.2 17.0 %collective-permute-done.4 = bf16[256,2048]{1,0:T(8,128)(2,1)} collective-permute-done((bf16[256,2048]{1,0:T(8,128)(2,1)S(1)}, bf16[256,2048]{1,0:T(8,128)(2,1)}, u32[]{:S(2)}, u32[]{:S(2)}) %collective-permute-start.4) | collective-permute-done | bytes 1048608 | tf_op jit(solution)/shard_map/ppermute | solution.py:29
  94.3 17.2 %collective-permute-done.5 = bf16[256,2048]{1,0:T(8,128)(2,1)} collective-permute-done((bf16[256,2048]{1,0:T(8,128)(2,1)}, bf16[256,2048]{1,0:T(8,128)(2,1)}, u32[]{:S(2)}, u32[]{:S(2)}) %collective-permute-start.5) | collective-permute-done | bytes 1048608 | tf_op jit(solution)/shard_map/ppermute | solution.py:29
  111.4 7.3 copy.24
  118.8 9.8 %collective-permute-done.6 = bf16[256,2048]{1,0:T(8,128)(2,1)} collective-permute-done((bf16[256,2048]{1,0:T(8,128)(2,1)}, bf16[256,2048]{1,0:T(8,128)(2,1)}, u32[]{:S(2)}, u32[]{:S(2)}) %collective-permute-start.6) | collective-permute-done | bytes 1048608 | tf_op jit(solution)/shard_map/ppermute | solution.py:29
  128.7 17.1 %collective-permute-done.7 = bf16[256,2048]{1,0:T(8,128)(2,1)S(1)} collective-permute-done((bf16[256,2048]{1,0:T(8,128)(2,1)}, bf16[256,2048]{1,0:T(8,128)(2,1)S(1)}, u32[]{:S(2)}, u32[]{:S(2)}) %collective-permute-start.7) | collective-permute-done | bytes 1048608 | tf_op jit(solution)/shard_map/ppermute | solution.py:29
  145.8 1.0 copy-done.3
  146.8 16.9 %collective-permute-done.8 = bf16[256,2048]{1,0:T(8,128)(2,1)S(1)} collective-permute-done((bf16[256,2048]{1,0:T(8,128)(2,1)S(1)}, bf16[256,2048]{1,0:T(8,128)(2,1)S(1)}, u32[]{:S(2)}, u32[]{:S(2)}) %collective-permute-start.8) | collective-permute-done | bytes 1048608 | tf_op jit(solution)/shard_map/ppermute | solution.py:29
  163.7 1.0 copy-done.5
  164.7 16.9 %collective-permute-done.9 = bf16[256,2048]{1,0:T(8,128)(2,1)S(1)} collective-permute-done((bf16[256,2048]{1,0:T(8,128)(2,1)S(1)}, bf16[256,2048]{1,0:T(8,128)(2,1)S(1)}, u32[]{:S(2)}, u32[]{:S(2)}) %collective-permute-start.9) | collective-permute-done | bytes 1048608 | tf_op jit(solution)/shard_map/ppermute | solution.py:29
  181.6 1.0 copy-done.7
  182.6 16.9 %collective-permute-done.10 = bf16[256,2048]{1,0:T(8,128)(2,1)S(1)} collective-permute-done((bf16[256,2048]{1,0:T(8,128)(2,1)S(1)}, bf16[256,2048]{1,0:T(8,128)(2,1)S(1)}, u32[]{:S(2)}, u32[]{:S(2)}) %collective-permute-start.10) | collective-permute-done | bytes 1048608 | tf_op jit(solution)/shard_map/ppermute | solution.py:29
  199.5 1.0 copy-done.9
  200.5 16.9 %collective-permute-done.11 = bf16[256,2048]{1,0:T(8,128)(2,1)S(1)} collective-permute-done((bf16[256,2048]{1,0:T(8,128)(2,1)S(1)}, bf16[256,2048]{1,0:T(8,128)(2,1)S(1)}, u32[]{:S(2)}, u32[]{:S(2)}) %collective-permute-start.11) | collective-permute-done | bytes 1048608 | tf_op jit(solution)/shard_map/ppermute | solution.py:29
  217.4 1.0 copy-done.11
  218.4 16.9 %collective-permute-done.12 = bf16[256,2048]{1,0:T(8,128)(2,1)S(1)} collective-permute-done((bf16[256,2048]{1,0:T(8,128)(2,1)S(1)}, bf16[256,2048]{1,0:T(8,128)(2,1)S(1)}, u32[]{:S(2)}, u32[]{:S(2)}) %collective-permute-start.12) | collective-permute-done | bytes 1048608 | tf_op jit(solution)/shard_map/ppermute | solution.py:29
  235.3 1.0 copy-done.13
  236.3 17.0 %collective-permute-done.13 = bf16[256,2048]{1,0:T(8,128)(2,1)} collective-permute-done((bf16[256,2048]{1,0:T(8,128)(2,1)S(1)}, bf16[256,2048]{1,0:T(8,128)(2,1)}, u32[]{:S(2)}, u32[]{:S(2)}) %collective-permute-start.13) | collective-permute-done | bytes 1048608 | tf_op jit(solution)/shard_map/ppermute | solution.py:29
  253.4 11.8 %convolution_convert_fusion = bf16[2,512,4096]{2,1,0:T(8,128)(2,1)} fusion(bf16[2,512,512]{2,1,0:T(8,128)(2,1)} %bitcast.31, bf16[4096,2,512]{0,2,1:T(8,128)(2,1)} %bitcast.33), kind=kOutput, calls=%fused_computation.4 | convolution fusion | flops 4299161600 | bytes 17825792 | tf_op jit(solution)/shard_map/mbj,bjr->mbr/dot_general | solution.py:20
  265.2 5.3 collective-permute-done.14
  270.5 1.3 constant_dynamic-update-slice_fusion.31
  271.8 1.3 constant_dynamic-update-slice_fusion.30
  273.1 1.3 constant_dynamic-update-slice_fusion.29
  275.0 1.3 constant_dynamic-update-slice_fusion.23
  276.3 1.3 constant_dynamic-update-slice_fusion.22
  277.6 1.3 constant_dynamic-update-slice_fusion.21
  279.4 1.3 constant_dynamic-update-slice_fusion.15
  280.7 1.3 constant_dynamic-update-slice_fusion.14
  282.6 1.3 constant_dynamic-update-slice_fusion.7
  283.9 1.3 constant_dynamic-update-slice_fusion.6
  285.2 1.3 constant_dynamic-update-slice_fusion.5
  287.0 6.9 constant_dynamic-slice_fusion
  293.9 35.4 %divide_convert_fusion = (bf16[2048,1024]{1,0:T(8,128)(2,1)}, f32[2048,1024]{1,0:T(8,128)}, f32[2048,1024]{1,0:T(8,128)}) fusion(f32[2048,1024]{1,0:T(8,128)} %param.8, f32[2048,1024]{1,0:T(8,128)} %param.9, bf16[4096,2048]{1,0:T(8,128)(2,1)} %constant_dynamic-slice_fusion, bf16[4096,1024]{0,1:T(8,128)(2,1)} %bitcast.35), kind=kOutput, calls=%fused_computation.3 | convolution fusion | flops 17202937856 | bytes 62914560 | tf_op jit(solution)/shard_map/dot_general | solution.py:33
  329.4 25.8 %fusion.11 = f32[4096,2048]{1,0:T(8,128)} fusion(bf16[4096,1024]{0,1:T(8,128)(2,1)} %all-gather.6.cloned.1.call-done, bf16[2048,1024]{0,1:T(8,128)(2,1)} %copy.24), kind=kOutput, calls=%fused_computation.46 | convolution fusion | flops 17179869184 | bytes 46137344 | tf_op jit(solution)/shard_map/dot_general | solution.py:56
  355.2 9.9 %all-to-all-start = ((bf16[2,2048,2048]{2,1,0:T(8,128)(2,1)}), bf16[2,2048,2048]{2,1,0:T(8,128)(2,1)}, u32[]{:S(2)}, u32[]{:S(2)}) async-start(bf16[2,2048,2048]{2,1,0:T(8,128)(2,1)} %bitcast.27), calls=%async_computation | async-start | bytes 33554432 | tf_op jit(solution)/shard_map/all_to_all | solution.py:41
  365.1 7.0 fusion.6
  372.5 1.1 bitcast_add_fusion
  373.6 237.2 %all-to-all-done = bf16[2,2048,2048]{2,1,0:T(8,128)(2,1)} async-done(((bf16[2,2048,2048]{2,1,0:T(8,128)(2,1)}), bf16[2,2048,2048]{2,1,0:T(8,128)(2,1)}, u32[]{:S(2)}, u32[]{:S(2)}) %all-to-all-start) | async-done | bytes 16777248 | tf_op jit(solution)/shard_map/all_to_all | solution.py:41
  610.8 22.6 %copy.23 = bf16[2048,2,2048]{0,2,1:T(8,128)(2,1)} copy(bf16[2048,2,2048]{2,0,1:T(8,128)(2,1)} %bitcast.1) | data formatting | bytes 33554432 | tf_op jit(solution)/shard_map/all_to_all | solution.py:41
  633.4 23.0 %convolution_convert_fusion.1 = bf16[2048,1024]{0,1:T(8,128)(2,1)S(1)} fusion(bf16[2048,4096]{0,1:T(8,128)(2,1)} %bitcast.29, bf16[4096,1024]{1,0:T(8,128)(2,1)} %all-gather.8.cloned.1.call-done), kind=kOutput, calls=%fused_computation.7 | convolution fusion | flops 17181966336 | bytes 29360128 | tf_op jit(solution)/shard_map/dot_general | solution.py:42
  656.4 5.6 fusion.12
  662.0 9.2 %copy.30 = f32[2048,1024]{1,0:T(8,128)} copy(f32[2048,1024]{0,1:T(8,128)} %bitcast.28) | data formatting | bytes 16777216
  671.3 183.5 %reduce-scatter.2.cloned.1.call-done = f32[256,2048]{1,0:T(8,128)} async-done(((f32[4096,2048]{1,0:T(8,128)}), f32[256,2048]{1,0:T(8,128)}) %reduce-scatter.2.cloned.1.call-update) | async-done | bytes 2097168 | tf_op jit(solution)/shard_map/reduce_scatter | solution.py:55
  854.8 3.3 multiply_add_fusion.1
  (77 shorter events, 3.1 us)
Async XLA Ops:
  7.2 246.1 %all-gather.4.cloned.1.call-start = ((), (), s32[]{:S(2)}) async-start(), calls=%async_computation.2 | async-start | bytes 1572864 | tf_op jit(solution)/shard_map/all_gather | solution.py:16
  7.2 18.2 %collective-permute-start = (bf16[256,2048]{1,0:T(8,128)(2,1)}, bf16[256,2048]{1,0:T(8,128)(2,1)S(1)}, u32[]{:S(2)}, u32[]{:S(2)}) collective-permute-start(bf16[256,2048]{1,0:T(8,128)(2,1)} %param.10), channel_id=1, source_target_pairs={{0,2},{2,4},{4,6},{6,8},{8,10},{10,12},{12,14},{14,16},{16,18},{18... | collective-permute-start | bytes 3145736 | tf_op jit(solution)/shard_map/ppermute | solution.py:29
  25.4 16.9 %collective-permute-start.1 = (bf16[256,2048]{1,0:T(8,128)(2,1)S(1)}, bf16[256,2048]{1,0:T(8,128)(2,1)S(1)}, u32[]{:S(2)}, u32[]{:S(2)}) collective-permute-start(bf16[256,2048]{1,0:T(8,128)(2,1)S(1)} %collective-permute-done), channel_id=1, source_target_pairs={{0,2},{2,4},{4,6},{6,8},{8,10},{10,12},{12,14},{14,16},{16,18},{18... | collective-permute-start | bytes 3145736 | tf_op jit(solution)/shard_map/ppermute | solution.py:29
  42.4 16.9 %collective-permute-start.2 = (bf16[256,2048]{1,0:T(8,128)(2,1)S(1)}, bf16[256,2048]{1,0:T(8,128)(2,1)S(1)}, u32[]{:S(2)}, u32[]{:S(2)}) collective-permute-start(bf16[256,2048]{1,0:T(8,128)(2,1)S(1)} %collective-permute-done.1), channel_id=1, source_target_pairs={{0,2},{2,4},{4,6},{6,8},{8,10},{10,12},{12,14},{14,16},{16,18},{18... | collective-permute-start | bytes 3145736 | tf_op jit(solution)/shard_map/ppermute | solution.py:29
  59.3 16.9 %collective-permute-start.3 = (bf16[256,2048]{1,0:T(8,128)(2,1)S(1)}, bf16[256,2048]{1,0:T(8,128)(2,1)S(1)}, u32[]{:S(2)}, u32[]{:S(2)}) collective-permute-start(bf16[256,2048]{1,0:T(8,128)(2,1)S(1)} %collective-permute-done.2), channel_id=1, source_target_pairs={{0,2},{2,4},{4,6},{6,8},{8,10},{10,12},{12,14},{14,16},{16,18},{18... | collective-permute-start | bytes 3145736 | tf_op jit(solution)/shard_map/ppermute | solution.py:29
  76.2 1.0 copy-start.1
  77.2 17.0 %collective-permute-start.4 = (bf16[256,2048]{1,0:T(8,128)(2,1)S(1)}, bf16[256,2048]{1,0:T(8,128)(2,1)}, u32[]{:S(2)}, u32[]{:S(2)}) collective-permute-start(bf16[256,2048]{1,0:T(8,128)(2,1)S(1)} %collective-permute-done.3), channel_id=1, source_target_pairs={{0,2},{2,4},{4,6},{6,8},{8,10},{10,12},{12,14},{14,16},{16,18},{18... | collective-permute-start | bytes 3145736 | tf_op jit(solution)/shard_map/ppermute | solution.py:29
  94.2 17.2 %collective-permute-start.5 = (bf16[256,2048]{1,0:T(8,128)(2,1)}, bf16[256,2048]{1,0:T(8,128)(2,1)}, u32[]{:S(2)}, u32[]{:S(2)}) collective-permute-start(bf16[256,2048]{1,0:T(8,128)(2,1)} %collective-permute-done.4), channel_id=1, source_target_pairs={{0,2},{2,4},{4,6},{6,8},{8,10},{10,12},{12,14},{14,16},{16,18},{18... | collective-permute-start | bytes 3145736 | tf_op jit(solution)/shard_map/ppermute | solution.py:29
  94.2 159.1 %all-gather.6.cloned.1.call-start = ((), (), s32[]{:S(2)}) async-start(), calls=%async_computation.3 | async-start | bytes 12582912 | tf_op jit(solution)/shard_map/all_gather | solution.py:18
  111.4 17.2 %collective-permute-start.6 = (bf16[256,2048]{1,0:T(8,128)(2,1)}, bf16[256,2048]{1,0:T(8,128)(2,1)}, u32[]{:S(2)}, u32[]{:S(2)}) collective-permute-start(bf16[256,2048]{1,0:T(8,128)(2,1)} %collective-permute-done.5), channel_id=1, source_target_pairs={{0,2},{2,4},{4,6},{6,8},{8,10},{10,12},{12,14},{14,16},{16,18},{18... | collective-permute-start | bytes 3145736 | tf_op jit(solution)/shard_map/ppermute | solution.py:29
  118.8 514.6 %all-gather.8.cloned.1.call-start = ((), (), s32[]{:S(2)}) async-start(), calls=%async_computation.4 | async-start | bytes 12582912 | tf_op jit(solution)/shard_map/all_gather | solution.py:44
  128.7 17.1 %collective-permute-start.7 = (bf16[256,2048]{1,0:T(8,128)(2,1)}, bf16[256,2048]{1,0:T(8,128)(2,1)S(1)}, u32[]{:S(2)}, u32[]{:S(2)}) collective-permute-start(bf16[256,2048]{1,0:T(8,128)(2,1)} %collective-permute-done.6), channel_id=1, source_target_pairs={{0,2},{2,4},{4,6},{6,8},{8,10},{10,12},{12,14},{14,16},{16,18},{18... | collective-permute-start | bytes 3145736 | tf_op jit(solution)/shard_map/ppermute | solution.py:29
  145.8 1.0 copy-start.3
  146.8 16.9 %collective-permute-start.8 = (bf16[256,2048]{1,0:T(8,128)(2,1)S(1)}, bf16[256,2048]{1,0:T(8,128)(2,1)S(1)}, u32[]{:S(2)}, u32[]{:S(2)}) collective-permute-start(bf16[256,2048]{1,0:T(8,128)(2,1)S(1)} %collective-permute-done.7), channel_id=1, source_target_pairs={{0,2},{2,4},{4,6},{6,8},{8,10},{10,12},{12,14},{14,16},{16,18},{18... | collective-permute-start | bytes 3145736 | tf_op jit(solution)/shard_map/ppermute | solution.py:29
  163.7 1.0 copy-start.5
  164.7 16.9 %collective-permute-start.9 = (bf16[256,2048]{1,0:T(8,128)(2,1)S(1)}, bf16[256,2048]{1,0:T(8,128)(2,1)S(1)}, u32[]{:S(2)}, u32[]{:S(2)}) collective-permute-start(bf16[256,2048]{1,0:T(8,128)(2,1)S(1)} %collective-permute-done.8), channel_id=1, source_target_pairs={{0,2},{2,4},{4,6},{6,8},{8,10},{10,12},{12,14},{14,16},{16,18},{18... | collective-permute-start | bytes 3145736 | tf_op jit(solution)/shard_map/ppermute | solution.py:29
  181.6 1.0 copy-start.7
  182.6 16.9 %collective-permute-start.10 = (bf16[256,2048]{1,0:T(8,128)(2,1)S(1)}, bf16[256,2048]{1,0:T(8,128)(2,1)S(1)}, u32[]{:S(2)}, u32[]{:S(2)}) collective-permute-start(bf16[256,2048]{1,0:T(8,128)(2,1)S(1)} %collective-permute-done.9), channel_id=1, source_target_pairs={{0,2},{2,4},{4,6},{6,8},{8,10},{10,12},{12,14},{14,16},{16,18},{18... | collective-permute-start | bytes 3145736 | tf_op jit(solution)/shard_map/ppermute | solution.py:29
  199.5 1.0 copy-start.9
  200.5 16.9 %collective-permute-start.11 = (bf16[256,2048]{1,0:T(8,128)(2,1)S(1)}, bf16[256,2048]{1,0:T(8,128)(2,1)S(1)}, u32[]{:S(2)}, u32[]{:S(2)}) collective-permute-start(bf16[256,2048]{1,0:T(8,128)(2,1)S(1)} %collective-permute-done.10), channel_id=1, source_target_pairs={{0,2},{2,4},{4,6},{6,8},{8,10},{10,12},{12,14},{14,16},{16,18},{18... | collective-permute-start | bytes 3145736 | tf_op jit(solution)/shard_map/ppermute | solution.py:29
  217.4 1.0 copy-start.11
  218.4 16.9 %collective-permute-start.12 = (bf16[256,2048]{1,0:T(8,128)(2,1)S(1)}, bf16[256,2048]{1,0:T(8,128)(2,1)S(1)}, u32[]{:S(2)}, u32[]{:S(2)}) collective-permute-start(bf16[256,2048]{1,0:T(8,128)(2,1)S(1)} %collective-permute-done.11), channel_id=1, source_target_pairs={{0,2},{2,4},{4,6},{6,8},{8,10},{10,12},{12,14},{14,16},{16,18},{18... | collective-permute-start | bytes 3145736 | tf_op jit(solution)/shard_map/ppermute | solution.py:29
  235.3 1.0 copy-start.13
  236.3 17.0 %collective-permute-start.13 = (bf16[256,2048]{1,0:T(8,128)(2,1)S(1)}, bf16[256,2048]{1,0:T(8,128)(2,1)}, u32[]{:S(2)}, u32[]{:S(2)}) collective-permute-start(bf16[256,2048]{1,0:T(8,128)(2,1)S(1)} %collective-permute-done.12), channel_id=1, source_target_pairs={{0,2},{2,4},{4,6},{6,8},{8,10},{10,12},{12,14},{14,16},{16,18},{18... | collective-permute-start | bytes 3145736 | tf_op jit(solution)/shard_map/ppermute | solution.py:29
  253.3 17.2 %collective-permute-start.14 = (bf16[256,2048]{1,0:T(8,128)(2,1)}, bf16[256,2048]{1,0:T(8,128)(2,1)}, u32[]{:S(2)}, u32[]{:S(2)}) collective-permute-start(bf16[256,2048]{1,0:T(8,128)(2,1)} %collective-permute-done.13), channel_id=1, source_target_pairs={{0,2},{2,4},{4,6},{6,8},{8,10},{10,12},{12,14},{14,16},{16,18},{18... | collective-permute-start | bytes 3145736 | tf_op jit(solution)/shard_map/ppermute | solution.py:29
  253.3 21.1 %copy-start.12 = (bf16[256,2048]{1,0:T(8,128)(2,1)S(1)}, bf16[256,2048]{1,0:T(8,128)(2,1)}, u32[]{:S(2)}) copy-start(bf16[256,2048]{1,0:T(8,128)(2,1)} %copy-done.11) | copy-start | bytes 3145732
  253.3 21.2 %copy-start.10 = (bf16[256,2048]{1,0:T(8,128)(2,1)S(1)}, bf16[256,2048]{1,0:T(8,128)(2,1)}, u32[]{:S(2)}) copy-start(bf16[256,2048]{1,0:T(8,128)(2,1)} %copy-done.9) | copy-start | bytes 3145732
  253.3 21.3 %copy-start.8 = (bf16[256,2048]{1,0:T(8,128)(2,1)S(1)}, bf16[256,2048]{1,0:T(8,128)(2,1)}, u32[]{:S(2)}) copy-start(bf16[256,2048]{1,0:T(8,128)(2,1)} %copy-done.7) | copy-start | bytes 3145732
  253.3 21.5 %copy-start.6 = (bf16[256,2048]{1,0:T(8,128)(2,1)S(1)}, bf16[256,2048]{1,0:T(8,128)(2,1)}, u32[]{:S(2)}) copy-start(bf16[256,2048]{1,0:T(8,128)(2,1)} %copy-done.5) | copy-start | bytes 3145732
  253.3 21.6 %copy-start.4 = (bf16[256,2048]{1,0:T(8,128)(2,1)S(1)}, bf16[256,2048]{1,0:T(8,128)(2,1)}, u32[]{:S(2)}) copy-start(bf16[256,2048]{1,0:T(8,128)(2,1)} %copy-done.3) | copy-start | bytes 3145732
  253.3 25.6 %copy-start.2 = (bf16[256,2048]{1,0:T(8,128)(2,1)S(1)}, bf16[256,2048]{1,0:T(8,128)(2,1)}, u32[]{:S(2)}) copy-start(bf16[256,2048]{1,0:T(8,128)(2,1)} %copy-done.1) | copy-start | bytes 3145732
  253.4 25.9 %copy-start = (bf16[256,2048]{1,0:T(8,128)(2,1)S(1)}, bf16[256,2048]{1,0:T(8,128)(2,1)}, u32[]{:S(2)}) copy-start(bf16[256,2048]{1,0:T(8,128)(2,1)} %param.10) | copy-start | bytes 3145732
  265.2 16.8 %copy-start.14 = (bf16[256,2048]{1,0:T(8,128)(2,1)S(1)}, bf16[256,2048]{1,0:T(8,128)(2,1)}, u32[]{:S(2)}) copy-start(bf16[256,2048]{1,0:T(8,128)(2,1)} %copy-done.13) | copy-start | bytes 3145732
  329.3 525.5 %reduce-scatter.2.cloned.1.call-start = ((), (), s32[]{:S(2)}) async-start(), calls=%async_computation.5 | async-start | bytes 35651584 | tf_op jit(solution)/shard_map/reduce_scatter | solution.py:55
  355.2 17.3 %copy-start.17 = (f32[1024,256]{1,0:T(8,128)S(1)}, f32[1024,256]{1,0:T(8,128)}, u32[]{:S(2)}) copy-start(f32[1024,256]{1,0:T(8,128)} %param.13) | copy-start | bytes 3145732
  355.2 255.6 %all-to-all-start = ((bf16[2,2048,2048]{2,1,0:T(8,128)(2,1)}), bf16[2,2048,2048]{2,1,0:T(8,128)(2,1)}, u32[]{:S(2)}, u32[]{:S(2)}) async-start(bf16[2,2048,2048]{2,1,0:T(8,128)(2,1)} %bitcast.27), calls=%async_computation | async-start | bytes 33554432 | tf_op jit(solution)/shard_map/all_to_all | solution.py:41
  633.4 23.0 %copy-start.15 = (bf16[1024,512]{1,0:T(8,128)(2,1)S(1)}, bf16[1024,512]{1,0:T(8,128)(2,1)}, u32[]{:S(2)}) copy-start(bf16[1024,512]{1,0:T(8,128)(2,1)} %all-gather.4.cloned.1.call-done) | copy-start | bytes 3145732
  656.4 198.4 %copy-start.16 = (f32[256,2048]{1,0:T(8,128)S(1)}, f32[256,2048]{1,0:T(8,128)}, u32[]{:S(2)}) copy-start(f32[256,2048]{1,0:T(8,128)} %param.12) | copy-start | bytes 6291460
Sparse Core Ops, SparseCore 0:
  94.3 22.8 all-gather.3
  118.9 105.5 all-gather.5
  329.4 173.0 all-gather.7
  506.6 348.1 reduce-scatter.1
